TPU v7x, 128 devices: a whole 4x4x4 slice. The times are simulated.
128 devices in a mesh: expert: 8 (over z, core), shard: 16 (over y, x).
Axes of the slice: x: 4, y: 4, z: 4, core: 2. Of those that a mesh axis runs over, the one named last changes fastest.
Arguments:
- master_down: float32 [16, 6400, 4096], P('expert', None, 'shard'), may hold values from -0.109375 to 0.109375
- second_down: bfloat16 [16, 6400, 4096], P('expert', None, 'shard'), may hold values from -0.0390625 to 0.0390625
- router_weight: float32 [4096, 16], P('shard', 'expert'), may hold values from -0.09375 to 0.09375
- router_gain: float32 [4096], P('shard'), may hold values from 0.25 to 1.75
Outputs:
- final_down: bfloat16 [16, 6400, 4096], P('expert', 'shard')
- scale_down: float32 [16, 6400], P('expert', 'shard')
- serve_router: bfloat16 [4096, 16], replicated
All inputs are finite; a program needn't handle non-finite values.
Results may differ from a plain program's by a relative error of at most 0.001.
Values may be sent and summed in bfloat16 or wider, within the bound.
A program may use at most 128 MiB of HBM per device.

v0:
```python
import jax
import jax.numpy as jnp
from jax import lax
from jax.sharding import Mesh
from jax.sharding import PartitionSpec as P

EXPERT = ("expert_0", "expert_1")


def from_everyone(x, axis):
    size = lax.axis_size(axis)
    return lax.all_to_all(jnp.broadcast_to(x[None], (size, *x.shape)), axis, 0, 0, tiled=True)


def taken_together(x, axis):
    everything = from_everyone(x, axis)
    return jnp.sum(everything, axis=0)


def cut_along(x, dim, size):
    shape = x.shape
    parts = x.reshape(*shape[:dim], size, shape[dim] // size, *shape[dim + 1 :])
    return jnp.moveaxis(parts, dim, 0)


def cut_rows(length, count):
    hop = length // count
    if hop >= 8:
        hop -= hop % 8
    return [hop * k for k in range(1, count)]


def joined_along(parts, dim):
    parts = jnp.moveaxis(parts, 0, dim)
    shape = parts.shape
    return parts.reshape(*shape[:dim], shape[dim] * shape[dim + 1], *shape[dim + 2 :])


def several_exchanges(x, axis, pieces, split_dim, concat_dim):
    parts = cut_along(x, split_dim, lax.axis_size(axis))
    widest = max(range(1, max(2, parts.ndim - 1)), key=lambda d: parts.shape[d])
    done = []
    for share in jnp.split(parts, cut_rows(parts.shape[widest], pieces), axis=widest):
        if share.size:
            done.append(lax.all_to_all(share, axis, split_axis=0, concat_axis=0, tiled=True))
    return joined_along(jnp.concatenate(done, axis=widest), concat_dim)


def collect(x, axis, dim):
    parts = from_everyone(x, axis)
    return joined_along(parts, dim)


def all_blocks(x, axes, sequence):
    parts = x
    for k in sequence:
        parts = lax.all_gather(parts, axes[k])
    done = sequence[::-1]
    back = [done.index(k) for k in range(len(axes))]
    parts = parts.transpose(*back, *range(len(axes), parts.ndim))
    return parts.reshape(-1, *x.shape)


def gathered_by_axis(x, axes, sequence, dim):
    return joined_along(all_blocks(x, axes, sequence), dim)


def local(master_down, second_down, router_weight, router_gain):
    merged_down = master_down + second_down.astype(jnp.float32)
    total_down = taken_together(jnp.sum(merged_down * merged_down, axis=2), "shard")
    scale_down = jnp.sqrt(total_down)
    narrow_down = (merged_down / jnp.expand_dims(scale_down, 2)).astype(jnp.bfloat16)
    final_down = several_exchanges(narrow_down, "shard", 2, 1, 2)
    scale_down = lax.dynamic_slice_in_dim(
        scale_down, lax.axis_index("shard") * final_down.shape[1], final_down.shape[1], axis=1
    )
    part_router = (router_weight * router_gain[:, None]).astype(jnp.bfloat16)
    row_router = collect(part_router, "shard", 0)
    serve_router = gathered_by_axis(row_router, ("expert_0", "expert_1"), (0, 1), 1)
    return (final_down, scale_down, serve_router)


def solution(mesh):
    finer = Mesh(mesh.devices.reshape(4, 2, mesh.shape["shard"]), ("expert_0", "expert_1", "shard"))
    placed = (P(EXPERT, None, "shard"), P(EXPERT, None, "shard"), P("shard", EXPERT), P("shard"))
    return jax.shard_map(
        local,
        mesh=finer,
        in_specs=placed,
        out_specs=(P(EXPERT, "shard", None), P(EXPERT, "shard"), P()),
        check_vma=False,
    )
```

profile of v0, /device:TPU:0, one launch (start us, length us, event | category | flops | bytes accessed | tf_op | source)
XLA Modules:
  0.0 156.0 jit_solution(14514300094531729462)
XLA Ops:
  0.6 0.0 copy-start
  0.6 0.0 copy-start.1
  0.7 8.4 %multiply_reduce_fusion = f32[2,6400]{1,0:T(2,128)S(1)} fusion(f32[2,6400,256]{2,1,0:T(8,128)} %param.4, bf16[2,6400,256]{2,1,0:T(8,128)(2,1)} %param.5), kind=kLoop, calls=%fused_computation.1 | loop fusion | flops 13094400 | bytes 19712000 | tf_op jit(solution)/shard_map/reduce_sum | solution.py:70
  9.1 1.1 broadcast_in_dim.4
  10.2 7.1 %all-to-all-start = ((f32[16,2,6400]{2,1,0:T(2,128)}), f32[16,2,6400]{2,1,0:T(2,128)S(1)}, u32[]{:S(2)}, u32[]{:S(2)}) async-start(f32[16,2,6400]{2,1,0:T(2,128)} %broadcast_in_dim.4), calls=%async_computation | async-start | bytes 1638400 | tf_op jit(solution)/shard_map/all_to_all | solution.py:12
  17.3 0.0 copy-done
  17.4 0.0 copy-done.1
  17.4 14.9 %all-to-all-done = f32[16,2,6400]{2,1,0:T(2,128)S(1)} async-done(((f32[16,2,6400]{2,1,0:T(2,128)}), f32[16,2,6400]{2,1,0:T(2,128)S(1)}, u32[]{:S(2)}, u32[]{:S(2)}) %all-to-all-start) | async-done | bytes 819232 | tf_op jit(solution)/shard_map/all_to_all | solution.py:12
  32.3 0.6 broadcast_in_dim.5
  32.9 3.5 %all-to-all-start.3 = ((bf16[16,256,2]{1,2,0:T(2,128)(2,1)}), bf16[16,256,2]{1,2,0:T(2,128)(2,1)S(1)}, u32[]{:S(2)}, u32[]{:S(2)}) async-start(bf16[16,256,2]{1,2,0:T(2,128)(2,1)} %broadcast_in_dim.5), calls=%async_computation.3 | async-start | bytes 32768 | tf_op jit(solution)/shard_map/all_to_all | solution.py:12
  36.4 0.3 reduce_sum.19
  36.6 0.1 sqrt.7
  36.7 7.7 %divide_convert_fusion = bf16[2,6400,256]{2,1,0:T(8,128)(2,1)S(1)} fusion(f32[2,6400,256]{2,1,0:T(8,128)} %param.4, bf16[2,6400,256]{2,1,0:T(8,128)(2,1)} %param.5, f32[2,6400]{1,0:T(2,128)S(1)} %sqrt.7), kind=kLoop, calls=%fused_computation | loop fusion | flops 13107200 | bytes 26265600 | tf_op jit(solution)/shard_map/convert_element_type | solution.py:72
  44.4 2.1 %fusion = (bf16[16,2,200,256]{3,2,0,1:T(8,128)(2,1)S(1)}, bf16[16,2,200,256]{3,2,0,1:T(8,128)(2,1)}) fusion(bf16[16,2,400,256]{3,2,0,1:T(8,128)(2,1)S(1)} %bitcast.16), kind=kLoop, calls=%fused_computation.6 | loop fusion | bytes 13107200 | tf_op jit(solution)/shard_map/split | solution.py:43
  46.6 1.9 %copy.22 = bf16[16,2,200,256]{3,2,1,0:T(8,128)(2,1)} copy(bf16[16,2,200,256]{3,2,0,1:T(8,128)(2,1)S(1)} %get-tuple-element.3) | data formatting | bytes 6553600 | tf_op jit(solution)/shard_map/split | solution.py:43
  48.5 0.0 all-to-all-done.3
  48.5 7.2 %all-to-all-start.1 = ((bf16[16,2,200,256]{3,2,1,0:T(8,128)(2,1)}), bf16[16,2,200,256]{3,2,1,0:T(8,128)(2,1)S(1)}, u32[]{:S(2)}, u32[]{:S(2)}) async-start(bf16[16,2,200,256]{3,2,1,0:T(8,128)(2,1)} %copy.22), calls=%async_computation.1 | async-start | bytes 6553600 | tf_op jit(solution)/shard_map/all_to_all | solution.py:45
  55.7 3.8 %copy.23 = bf16[16,2,200,256]{3,2,1,0:T(8,128)(2,1)} copy(bf16[16,2,200,256]{3,2,0,1:T(8,128)(2,1)} %get-tuple-element.4) | data formatting | bytes 6553600 | tf_op jit(solution)/shard_map/split | solution.py:43
  59.5 41.0 %all-to-all-done.1 = bf16[16,2,200,256]{3,2,1,0:T(8,128)(2,1)S(1)} async-done(((bf16[16,2,200,256]{3,2,1,0:T(8,128)(2,1)}), bf16[16,2,200,256]{3,2,1,0:T(8,128)(2,1)S(1)}, u32[]{:S(2)}, u32[]{:S(2)}) %all-to-all-start.1) | async-done | bytes 3276832 | tf_op jit(solution)/shard_map/all_to_all | solution.py:45
  100.5 4.5 %all-to-all-start.2 = ((bf16[16,2,200,256]{3,2,1,0:T(8,128)(2,1)}), bf16[16,2,200,256]{3,2,1,0:T(8,128)(2,1)}, u32[]{:S(2)}, u32[]{:S(2)}) async-start(bf16[16,2,200,256]{3,2,1,0:T(8,128)(2,1)} %copy.23), calls=%async_computation.2 | async-start | bytes 6553600 | tf_op jit(solution)/shard_map/all_to_all | solution.py:45
  105.0 13.1 %all_gather.9 = bf16[4,4096,2]{1,2,0:T(2,128)(2,1)S(1)} all-gather(bf16[1,4096,2]{1,2,0:T(2,128)(2,1)S(1)} %bitcast.20), channel_id=1, replica_groups=mesh['expert_0'=4,'expert_1'=2,'shard'=16] {'expert_0'}, dimensions={0}, use_global_device_ids=true | all-gather | bytes 81920 | tf_op jit(solution)/shard_map/all_gather | solution.py:57
  118.1 1.9 %all-gather = bf16[8,4096,2]{1,2,0:T(2,128)(2,1)S(1)} all-gather(bf16[4,4096,2]{1,2,0:T(2,128)(2,1)S(1)} %all_gather.9), channel_id=2, replica_groups=mesh['expert_0'=4,'expert_1'=2,'shard'=16] {'expert_1'}, dimensions={0}, use_global_device_ids=true | all-gather | bytes 196608 | tf_op jit(solution)/shard_map/all_gather | solution.py:57
  120.0 0.1 copy.25
  120.1 0.7 reshape.27
  120.8 0.7 constant_dynamic-slice_fusion
  121.5 28.4 %all-to-all-done.2 = bf16[16,2,200,256]{3,2,1,0:T(8,128)(2,1)} async-done(((bf16[16,2,200,256]{3,2,1,0:T(8,128)(2,1)}), bf16[16,2,200,256]{3,2,1,0:T(8,128)(2,1)}, u32[]{:S(2)}, u32[]{:S(2)}) %all-to-all-start.2) | async-done | bytes 3276832 | tf_op jit(solution)/shard_map/all_to_all | solution.py:45
  149.9 2.5 %maximum_bitcast_fusion = bf16[16,2,50,8,256]{4,3,2,1,0:T(8,128)(2,1)S(1)} fusion(bf16[16,2,200,256]{3,2,1,0:T(8,128)(2,1)} %all-to-all-done.2, bf16[16,2,200,256]{3,2,1,0:T(8,128)(2,1)S(1)} %all-to-all-done.1), kind=kLoop, calls=%fused_computation.3 | loop fusion | flops 13107200 | bytes 13107200
  152.3 3.7 %copy.27 = bf16[16,2,50,8,256]{4,3,0,2,1:T(8,128)(2,1)} copy(bf16[16,2,50,8,256]{4,3,2,1,0:T(8,128)(2,1)S(1)} %maximum_bitcast_fusion) | data formatting | bytes 13107200 | tf_op jit(solution)/shard_map/reshape | solution.py:36
  (1 shorter events, 0.0 us)
Async XLA Ops:
  0.6 16.7 %copy-start = (f32[256,2]{0,1:T(2,128)S(1)}, f32[256,2]{0,1:T(2,128)}, u32[]{:S(2)}) copy-start(f32[256,2]{0,1:T(2,128)} %param.6) | copy-start | bytes 6148
  0.6 16.7 %copy-start.1 = (f32[256]{0:T(256)S(1)}, f32[256]{0:T(256)}, u32[]{:S(2)}) copy-start(f32[256]{0:T(256)} %param.7) | copy-start | bytes 3076
  10.2 22.1 %all-to-all-start = ((f32[16,2,6400]{2,1,0:T(2,128)}), f32[16,2,6400]{2,1,0:T(2,128)S(1)}, u32[]{:S(2)}, u32[]{:S(2)}) async-start(f32[16,2,6400]{2,1,0:T(2,128)} %broadcast_in_dim.4), calls=%async_computation | async-start | bytes 1638400 | tf_op jit(solution)/shard_map/all_to_all | solution.py:12
  32.9 15.6 %all-to-all-start.3 = ((bf16[16,256,2]{1,2,0:T(2,128)(2,1)}), bf16[16,256,2]{1,2,0:T(2,128)(2,1)S(1)}, u32[]{:S(2)}, u32[]{:S(2)}) async-start(bf16[16,256,2]{1,2,0:T(2,128)(2,1)} %broadcast_in_dim.5), calls=%async_computation.3 | async-start | bytes 32768 | tf_op jit(solution)/shard_map/all_to_all | solution.py:12
  48.5 52.0 %all-to-all-start.1 = ((bf16[16,2,200,256]{3,2,1,0:T(8,128)(2,1)}), bf16[16,2,200,256]{3,2,1,0:T(8,128)(2,1)S(1)}, u32[]{:S(2)}, u32[]{:S(2)}) async-start(bf16[16,2,200,256]{3,2,1,0:T(8,128)(2,1)} %copy.22), calls=%async_computation.1 | async-start | bytes 6553600 | tf_op jit(solution)/shard_map/all_to_all | solution.py:45
  100.5 49.4 %all-to-all-start.2 = ((bf16[16,2,200,256]{3,2,1,0:T(8,128)(2,1)}), bf16[16,2,200,256]{3,2,1,0:T(8,128)(2,1)}, u32[]{:S(2)}, u32[]{:S(2)}) async-start(bf16[16,2,200,256]{3,2,1,0:T(8,128)(2,1)} %copy.23), calls=%async_computation.2 | async-start | bytes 6553600 | tf_op jit(solution)/shard_map/all_to_all | solution.py:45
where the time goes:
time: 156 us
  waiting for transfers between devices  84.3 us (54%)
  starting transfers between devices  22.3 us (14%)
  other arithmetic  18.9 us (12%)
  blocking collectives  15 us (10%)
  local copies, waits for them, and re-layouts  14.8 us (9%)
    all_to_all x2, waiting for transfers between devices, several_exchanges(): lax.all_to_all(share, axis, split_axis=0, concat_axis=0, tiled=True)  69.4 us
    all_gather x2, blocking collectives, all_blocks(): parts = lax.all_gather(parts, axes[k])  15 us
    all_to_all x2, waiting for transfers between devices, from_everyone(): lax.all_to_all(jnp.broadcast_to(x[None], (size, *x.shape)), axis, 0, 0, t...  14.9 us
    all_to_all x2, starting transfers between devices, several_exchanges(): lax.all_to_all(share, axis, split_axis=0, concat_axis=0, tiled=True)  11.6 us
    all_to_all x2, starting transfers between devices, from_everyone(): lax.all_to_all(jnp.broadcast_to(x[None], (size, *x.shape)), axis, 0, 0, t...  10.6 us
    reduce_sum x1, other arithmetic, local(): jnp.sum(merged_down * merged_down, axis=2)  8.44 us
    split x3, local copies, waits for them, and re-layouts, several_exchanges(): jnp.split(parts, cut_rows(parts.shape[widest], pieces), axis=widest)  7.89 us
    convert_element_type x1, other arithmetic, local(): (merged_down / jnp.expand_dims(scale_down, 2)).astype(jnp.bfloat16)  7.74 us
  transfers between devices with their start and end apart: 4, of which 3 were waited for; matrix products, arithmetic and copies ran while one was open for 11% of the time, Pallas kernels for 0%

commit v1 on v0

v1 whole, which is shorter than its diff:
```python
import functools

import jax
import jax.numpy as jnp
from jax import lax
from jax.experimental import pallas as pl
from jax.experimental.pallas import tpu as pltpu
from jax.sharding import PartitionSpec as P

MESH = pl.DeviceIdType.MESH
SIDE = 4
LANES = 128

ROUNDS = (
    ((2, 3), (0, 1)),
    ((1, 3), (3, 1)),
    ((2, 1), (0, 3)),
    ((0, 2), (2, 0)),
    ((1, 0), (3, 2)),
    ((1, 2), (3, 0)),
    ((3, 3), (1, 1)),
    ((2, 2),),
)
DEPTH = 2


def pick(table, i):
    value = jnp.int32(0)
    for n, entry in enumerate(table):
        value = jnp.where(i == n, jnp.int32(entry), value)
    return value


def toward(shard, k):
    y, x = shard // SIDE, shard % SIDE
    return ((y + k // SIDE) % SIDE) * SIDE + (x + k % SIDE) % SIDE


def away(shard, k):
    y, x = shard // SIDE, shard % SIDE
    return ((y + SIDE - k // SIDE) % SIDE) * SIDE + (x + SIDE - k % SIDE) % SIDE


def kernel(
    shards, experts,
    master, second, weight_in, gain_in,
    final, scale, router,
    wide, narrow, ready, part, got, inverse, one_router, row_router, all_router, weight, gain,
    wide_sem, narrow_sem, weight_sem, gain_sem, part_send, part_recv, inv_send, inv_recv, row_send, row_recv, rt1_send, rt1_recv, rt2_send, rt2_recv,
):
    me = lax.axis_index("shard")
    mine = lax.axis_index("expert")
    held, rows, width = wide.shape[1:]
    groups = rows // 8

    def read(k):
        where = pl.ds(pl.multiple_of(toward(me, k) * rows, 16), rows)
        return (
            pltpu.make_async_copy(master.at[:, where, :], wide.at[k], wide_sem.at[k]),
            pltpu.make_async_copy(second.at[:, where, :], narrow.at[k], narrow_sem.at[k]),
        )

    @pl.loop(0, shards)
    def _(k):
        for copy in read(k):
            copy.start()

    read_weight = pltpu.make_async_copy(weight_in, weight, weight_sem)
    read_gain = pltpu.make_async_copy(gain_in, gain, gain_sem)
    read_weight.start()
    read_gain.start()

    barrier = pltpu.get_barrier_semaphore()

    @pl.loop(1, shards)
    def _(k):
        pl.semaphore_signal(barrier, inc=1, device_id={"shard": toward(me, k)}, device_id_type=MESH)

    @pl.loop(1, experts)
    def _(k):
        pl.semaphore_signal(barrier, inc=1, device_id={"expert": (mine + k) % experts}, device_id_type=MESH)

    read_weight.wait()
    read_gain.wait()
    mine_router = (weight[...] * gain[...]).astype(jnp.bfloat16)
    one_router[...] = mine_router
    columns = pl.ds(pl.multiple_of(me * width, LANES), width)
    row_router[:, columns] = mine_router
    pl.semaphore_wait(barrier, shards + experts - 2)

    def send_part(k):
        return pltpu.make_async_remote_copy(
            src_ref=part.at[k], dst_ref=got.at[k], send_sem=part_send.at[k], recv_sem=part_recv.at[k],
            device_id={"shard": toward(me, k)}, device_id_type=MESH,
        )

    def send_inverse(k):
        return pltpu.make_async_remote_copy(
            src_ref=inverse.at[0], dst_ref=inverse.at[k], send_sem=inv_send.at[k], recv_sem=inv_recv.at[k],
            device_id={"shard": away(me, k)}, device_id_type=MESH,
        )

    def send_rows(k):
        return pltpu.make_async_remote_copy(
            src_ref=ready.at[k], dst_ref=final.at[:, :, columns], send_sem=row_send.at[k], recv_sem=row_recv.at[k],
            device_id={"shard": toward(me, k)}, device_id_type=MESH,
        )

    def send_router(k):
        return pltpu.make_async_remote_copy(
            src_ref=one_router, dst_ref=row_router.at[:, columns], send_sem=rt1_send.at[k], recv_sem=rt1_recv.at[k],
            device_id={"shard": toward(me, k)}, device_id_type=MESH,
        )

    def send_row_router(k):
        return pltpu.make_async_remote_copy(
            src_ref=row_router, dst_ref=all_router.at[mine], send_sem=rt2_send.at[k], recv_sem=rt2_recv.at[k],
            device_id={"expert": (mine + k) % experts}, device_id_type=MESH,
        )

    lane = lax.broadcasted_iota(jnp.int32, (8, LANES), 1)
    sublane = lax.broadcasted_iota(jnp.int32, (8, LANES), 0)

    def squares(k):
        for copy in read(k):
            copy.wait()
        packed = jnp.zeros((8, LANES), jnp.float32)
        for e in range(held):
            for g in range(0, groups, 2):
                tall = pl.ds(8 * g, 16)
                merged = wide[k, e, tall, :] + narrow[k, e, tall, :].astype(jnp.float32)
                sums = jnp.sum(merged * merged, axis=1, keepdims=True)
                for h in range(2):
                    packed = jnp.where(lane == e * groups + g + h, sums[8 * h : 8 * h + 8], packed)
        part[k] = packed

    @pl.loop(1, shards)
    def _(k):
        squares(k)
        send_part(k).start()

    squares(0)

    def add(k, total):
        send_part(k).wait_recv()
        return total + got[k]

    total = lax.fori_loop(1, shards, add, part[0])
    root = jnp.sqrt(total)
    inverse[0] = 1.0 / root

    @pl.loop(1, shards)
    def _(k):
        send_inverse(k).start()

    @pl.loop(1, shards)
    def _(k):
        send_router(k).start()

    def scaled(k, store):
        factors = inverse[k]
        for e in range(held):
            for g in range(0, groups, 2):
                tall = pl.ds(8 * g, 16)
                merged = wide[k, e, tall, :] + narrow[k, e, tall, :].astype(jnp.float32)
                factor = jnp.concatenate(
                    [
                        jnp.broadcast_to(factors[:, e * groups + g + h : e * groups + g + h + 1], (8, width))
                        for h in range(2)
                    ],
                    axis=0,
                )
                store(e, tall, (merged * factor).astype(jnp.bfloat16))

    def scale_rows(k):
        def store(e, tall, value):
            ready[k, e, tall, :] = value

        scaled(k, store)

    offsets = [[dy * SIDE + dx for dy, dx in pair] for pair in ROUNDS]
    paired = [pair for pair in offsets if len(pair) == 2]
    firsts, seconds = [pair[0] for pair in paired], [pair[1] for pair in paired]
    alone = [pair[0] for pair in offsets if len(pair) == 1][0]

    def prepare(k):
        send_inverse(k).wait_recv()
        scale_rows(k)

    @pl.loop(0, len(paired))
    def _(p):
        @pl.loop(0, 2)
        def _(side):
            prepare(jnp.where(side == 0, pick(firsts, p), pick(seconds, p)))

        @pl.when(p >= DEPTH)
        def _():
            send_rows(pick(firsts, p - DEPTH)).wait_send()
            send_rows(pick(seconds, p - DEPTH)).wait_send()

        send_rows(pick(firsts, p)).start()
        send_rows(pick(seconds, p)).start()

    prepare(jnp.int32(alone))
    late = len(paired) - DEPTH
    send_rows(firsts[late]).wait_send()
    send_rows(seconds[late]).wait_send()
    send_rows(alone).start()

    @pl.loop(1, shards)
    def _(k):
        send_router(k).wait_recv()

    @pl.loop(1, experts)
    def _(k):
        send_row_router(k).start()

    all_router[mine] = row_router[...]

    def keep(e, tall, value):
        final[e, tall, columns] = value

    scaled(0, keep)

    for e in range(held):
        for c in range(0, rows, LANES):
            size = min(LANES, rows - c)
            spread = jnp.zeros((8, LANES), jnp.float32)
            for g in range(c // 8, (c + size) // 8):
                at = e * groups + g
                spread = jnp.where(lane // 8 == g - c // 8, jnp.broadcast_to(root[:, at : at + 1], (8, LANES)), spread)
            line = jnp.sum(jnp.where(sublane == lane % 8, spread, 0.0), axis=0, keepdims=True)
            scale[e : e + 1, c : c + size] = line[:, :size]

    @pl.loop(1, experts)
    def _(k):
        send_row_router(k).wait()

    router[...] = all_router[...].reshape(router.shape)

    @pl.loop(1, shards)
    def _(k):
        send_part(k).wait_send()
        send_inverse(k).wait_send()
        send_router(k).wait_send()
        send_rows(k).wait_recv()

    for p in range(late + 1, len(paired)):
        send_rows(firsts[p]).wait_send()
        send_rows(seconds[p]).wait_send()
    send_rows(alone).wait_send()


def hand_out_kernel(final, scale, router, final_out, scale_out, router_out, final_sem, scale_sem, router_sem):
    copies = [
        pltpu.make_async_copy(final, final_out, final_sem),
        pltpu.make_async_copy(scale, scale_out, scale_sem),
        pltpu.make_async_copy(router, router_out, router_sem),
    ]
    for copy in copies:
        copy.start()
    for copy in copies:
        copy.wait()


def hand_out(*arrays):
    return pl.pallas_call(
        hand_out_kernel,
        name="hand_out",
        out_shape=tuple(jax.ShapeDtypeStruct(x.shape, x.dtype) for x in arrays),
        in_specs=[pl.BlockSpec(memory_space=pltpu.VMEM)] * 3,
        out_specs=(pl.BlockSpec(memory_space=pltpu.HBM),) * 3,
        scratch_shapes=[pltpu.SemaphoreType.DMA] * 3,
        compiler_params=pltpu.CompilerParams(vmem_limit_bytes=8 * 1024 * 1024),
    )(*arrays)


def solution(mesh):
    shards, experts = mesh.shape["shard"], mesh.shape["expert"]

    def local(master, second, weight, gain):
        held, length, width = master.shape
        rows = length // shards
        dma = pltpu.SemaphoreType.DMA
        final, scale, router = pl.pallas_call(
            functools.partial(kernel, shards, experts),
            name="serve",
            out_shape=(
                jax.ShapeDtypeStruct((held, rows, width * shards), jnp.bfloat16),
                jax.ShapeDtypeStruct((held, rows), jnp.float32),
                jax.ShapeDtypeStruct((experts * held, width * shards), jnp.bfloat16),
            ),
            in_specs=[pl.BlockSpec(memory_space=pltpu.HBM)] * 4,
            out_specs=(pl.BlockSpec(memory_space=pltpu.VMEM),) * 3,
            scratch_shapes=[
                pltpu.VMEM((shards, held, rows, width), jnp.float32),
                pltpu.VMEM((shards, held, rows, width), jnp.bfloat16),
                pltpu.VMEM((shards, held, rows, width), jnp.bfloat16),
                pltpu.VMEM((shards, 8, LANES), jnp.float32),
                pltpu.VMEM((shards, 8, LANES), jnp.float32),
                pltpu.VMEM((shards, 8, LANES), jnp.float32),
                pltpu.VMEM((held, width), jnp.bfloat16),
                pltpu.VMEM((held, width * shards), jnp.bfloat16),
                pltpu.VMEM((experts, held, width * shards), jnp.bfloat16),
                pltpu.VMEM((held, width), jnp.float32),
                pltpu.VMEM((1, width), jnp.float32),
            ]
            + [dma((shards,))] * 2
            + [dma] * 2
            + [dma((shards,))] * 8
            + [dma((experts,))] * 2,
            compiler_params=pltpu.CompilerParams(
                collective_id=0, has_side_effects=True, vmem_limit_bytes=44 * 1024 * 1024
            ),
        )(*[pltpu.with_memory_space_constraint(x, pltpu.HBM) for x in (master, second, weight.T, gain[None, :])])
        final, scale, router = hand_out(final, scale, router)
        return final, scale, router.T

    return jax.shard_map(
        local,
        mesh=mesh,
        in_specs=(P("expert", None, "shard"), P("expert", None, "shard"), P("shard", "expert"), P("shard")),
        out_specs=(P("expert", "shard", None), P("expert", "shard"), P()),
        check_vma=False,
    )
```

time: 156 us -> 99.6 us (0.64)
  Pallas kernels: 0 us -> 98.9 us
  waiting for transfers between devices: 84.3 us -> 0 us
  starting transfers between devices: 22.3 us -> 0 us
  other arithmetic: 18.9 us -> 0 us
  blocking collectives: 15 us -> 0 us
  local copies, waits for them, and re-layouts: 14.8 us -> 0 us
    pallas_call x0 -> x2, Pallas kernels: none -> 98.9 us  [the longest x1 96 us: local(): pl.pallas_call(functools.partial(kernel, shards, experts), name='serve',...]
    all_to_all x4 -> x0, waiting for transfers between devices: 84.3 us -> none  [the longest x2 69.4 us: several_exchanges(): lax.all_to_all(share, axis, split_axis=0, concat_axis=0, tiled=True)]
    all_to_all x4 -> x0, starting transfers between devices: 22.3 us -> none  [the longest x2 11.6 us: several_exchanges(): lax.all_to_all(share, axis, split_axis=0, concat_axis=0, tiled=True)]
    all_gather x2 -> x0, blocking collectives: 15 us -> none  [all_blocks(): parts = lax.all_gather(parts, axes[k])]
    reduce_sum x2 -> x0, other arithmetic: 8.7 us -> none  [the longest x1 8.44 us: local(): jnp.sum(merged_down * merged_down, axis=2)]
    split x3 -> x0, local copies, waits for them, and re-layouts: 7.89 us -> none  [several_exchanges(): jnp.split(parts, cut_rows(parts.shape[widest], pieces), axis=widest)]
    convert_element_type x2 -> x0, other arithmetic: 7.74 us -> none  [the longest x1 7.74 us: local(): (merged_down / jnp.expand_dims(scale_down, 2)).astype(jnp.bfloat16)]
    reshape x2 -> x0, local copies, waits for them, and re-layouts: 4.4 us -> none  [joined_along(): parts.reshape(*shape[:dim], shape[dim] * shape[dim + 1], *shape[dim + 2:])]
  transfers between devices with their start and end apart: 4 -> 0, of which waited for: 3 -> 0; matrix products, arithmetic and copies ran while one was open for 11% -> 0% of each run, Pallas kernels for 0% -> 0%
where the time goes in v1:
time: 99.6 us; the launch traced here: 99.5 us
  Pallas kernels  98.9 us (99%)
    pallas_call x1, Pallas kernels, local(): pl.pallas_call(functools.partial(kernel, shards, experts), name='serve',...  96 us
    pallas_call x1, Pallas kernels, hand_out(): pl.pallas_call(hand_out_kernel, name='hand_out', out_shape=tuple((jax.Sha...  2.84 us

profile of v1, /device:TPU:0, one launch (start us, length us, event | category | flops | bytes accessed | tf_op | source)
XLA Modules:
  0.0 99.5 jit_solution(6831353963181988338)
XLA Ops:
  0.6 96.0 %serve.1 = (bf16[2,400,4096]{2,1,0:T(8,128)(2,1)S(1)}, f32[2,400]{1,0:T(2,128)S(1)}, bf16[16,4096]{1,0:T(8,128)(2,1)S(1)}) custom-call(f32[2,6400,256]{2,1,0:T(8,128)} %master.1, bf16[2,6400,256]{2,1,0:T(8,128)(2,1)} %second.1, f32[2,256]{1,0:T(2,128)} %bitcast.3, f32[1,256]{1,0:T(1,128)} %bitcast.4), custom_call_target="tpu_custom_call" | custom-call | tf_op jit(solution)/shard_map/serve/pallas_call | solution.py:285
  96.7 2.8 %hand_out.1 = (bf16[2,400,4096]{2,1,0:T(8,128)(2,1)}, f32[2,400]{1,0:T(2,128)}, bf16[16,4096]{1,0:T(8,128)(2,1)}) custom-call(bf16[2,400,4096]{2,1,0:T(8,128)(2,1)S(1)} %get-tuple-element.9.final, f32[2,400]{1,0:T(2,128)S(1)} %get-tuple-element.10.scale, bf16[16,4096]{1,0:T(8,128)(2,1)S(1)} %get-tuple-element.11.router), custom_call_target="tpu_custom_call" | custom-call | tf_op jit(solution)/shard_map/hand_out/pallas_call | solution.py:267

commit v2 on v1

--- a/solution.py
+++ b/solution.py
@@ -10,18 +10,12 @@
 MESH = pl.DeviceIdType.MESH
 SIDE = 4
 LANES = 128
-
-ROUNDS = (
-    ((2, 3), (0, 1)),
-    ((1, 3), (3, 1)),
-    ((2, 1), (0, 3)),
-    ((0, 2), (2, 0)),
-    ((1, 0), (3, 2)),
-    ((1, 2), (3, 0)),
-    ((3, 3), (1, 1)),
-    ((2, 2),),
-)
-DEPTH = 2
+HALF = LANES // 2
+
+PIECES = ((0, 1), (0, 3), (0, 2), (1, 1), (1, 3), (1, 2), (0, 0), (1, 0))
+ALONG = (1, 3, 2, 0)
+STRAIGHT = (1, 3, 2, 4, 12, 8)
+CUT = (0, 48, 96)
 
 
 def pick(table, i):
@@ -45,8 +39,9 @@
     shards, experts,
     master, second, weight_in, gain_in,
     final, scale, router,
-    wide, narrow, ready, part, got, inverse, one_router, row_router, all_router, weight, gain,
+    wide, narrow, ready, part, got, inverse, one_router, row_router, all_router, weight, gain, raw, stage,
     wide_sem, narrow_sem, weight_sem, gain_sem, part_send, part_recv, inv_send, inv_recv, row_send, row_recv, rt1_send, rt1_recv, rt2_send, rt2_recv,
+    raw_send, raw_recv, relay_send, relay_recv,
 ):
     me = lax.axis_index("shard")
     mine = lax.axis_index("expert")
@@ -86,7 +81,6 @@
     one_router[...] = mine_router
     columns = pl.ds(pl.multiple_of(me * width, LANES), width)
     row_router[:, columns] = mine_router
-    pl.semaphore_wait(barrier, shards + experts - 2)
 
     def send_part(k):
         return pltpu.make_async_remote_copy(
@@ -100,9 +94,38 @@
             device_id={"shard": away(me, k)}, device_id_type=MESH,
         )
 
-    def send_rows(k):
-        return pltpu.make_async_remote_copy(
-            src_ref=ready.at[k], dst_ref=final.at[:, :, columns], send_sem=row_send.at[k], recv_sem=row_recv.at[k],
+    def send_straight(k, e, early=False):
+        skip = CUT[2] if early else 0
+        part_rows = pl.ds(skip, rows - skip)
+        return pltpu.make_async_remote_copy(
+            src_ref=ready.at[k, e, part_rows], dst_ref=final.at[e, part_rows, columns],
+            send_sem=row_send.at[2 * k + e], recv_sem=row_recv.at[2 * k + e],
+            device_id={"shard": toward(me, k)}, device_id_type=MESH,
+        )
+
+    def send_relay(k, e):
+        return pltpu.make_async_remote_copy(
+            src_ref=ready.at[k, e], dst_ref=stage.at[k, e],
+            send_sem=relay_send.at[2 * k + e], recv_sem=relay_recv.at[2 * k + e],
+            device_id={"shard": toward(me, k % SIDE)}, device_id_type=MESH,
+        )
+
+    def forward(k, e):
+        origin = pl.ds(pl.multiple_of(away(me, k % SIDE) * width, LANES), width)
+        return pltpu.make_async_remote_copy(
+            src_ref=stage.at[k, e], dst_ref=final.at[e, :, origin],
+            send_sem=row_send.at[2 * k + e], recv_sem=row_recv.at[2 * k + e],
+            device_id={"shard": toward(me, k - k % SIDE)}, device_id_type=MESH,
+        )
+
+    def send_raw(n, part_number):
+        k = pick(STRAIGHT, n)
+        first, last = CUT[part_number], CUT[part_number + 1]
+        part_rows = pl.ds(first, last - first)
+        at = 2 * n + part_number
+        return pltpu.make_async_remote_copy(
+            src_ref=wide.at[k, 0, part_rows], dst_ref=raw.at[n, part_rows],
+            send_sem=raw_send.at[at], recv_sem=raw_recv.at[at],
             device_id={"shard": toward(me, k)}, device_id_type=MESH,
         )
 
@@ -131,15 +154,36 @@
                 merged = wide[k, e, tall, :] + narrow[k, e, tall, :].astype(jnp.float32)
                 sums = jnp.sum(merged * merged, axis=1, keepdims=True)
                 for h in range(2):
-                    packed = jnp.where(lane == e * groups + g + h, sums[8 * h : 8 * h + 8], packed)
+                    packed = jnp.where(lane == e * HALF + g + h, sums[8 * h : 8 * h + 8], packed)
         part[k] = packed
 
-    @pl.loop(1, shards)
+    @pl.loop(1, shards // 2)
+    def _(k):
+        squares(k)
+
+    pl.semaphore_wait(barrier, shards + experts - 2)
+
+    @pl.loop(1, shards // 2)
+    def _(k):
+        send_part(k).start()
+
+    @pl.loop(shards // 2, shards)
     def _(k):
         squares(k)
         send_part(k).start()
 
+    @pl.loop(0, len(STRAIGHT))
+    def _(n):
+        k = pick(STRAIGHT, n)
+        for g in range(0, CUT[2] // 8, 2):
+            tall = pl.ds(8 * g, 16)
+            wide[k, 0, tall, :] += narrow[k, 0, tall, :].astype(jnp.float32)
+
     squares(0)
+
+    @pl.loop(0, len(STRAIGHT))
+    def _(n):
+        send_raw(n, 0).start()
 
     def add(k, total):
         send_part(k).wait_recv()
@@ -153,59 +197,54 @@
     def _(k):
         send_inverse(k).start()
 
+    @pl.loop(0, len(STRAIGHT))
+    def _(n):
+        send_raw(n, 1).start()
+
     @pl.loop(1, shards)
     def _(k):
         send_router(k).start()
 
-    def scaled(k, store):
-        factors = inverse[k]
-        for e in range(held):
-            for g in range(0, groups, 2):
-                tall = pl.ds(8 * g, 16)
-                merged = wide[k, e, tall, :] + narrow[k, e, tall, :].astype(jnp.float32)
-                factor = jnp.concatenate(
-                    [
-                        jnp.broadcast_to(factors[:, e * groups + g + h : e * groups + g + h + 1], (8, width))
-                        for h in range(2)
-                    ],
-                    axis=0,
-                )
-                store(e, tall, (merged * factor).astype(jnp.bfloat16))
-
-    def scale_rows(k):
-        def store(e, tall, value):
-            ready[k, e, tall, :] = value
-
-        scaled(k, store)
-
-    offsets = [[dy * SIDE + dx for dy, dx in pair] for pair in ROUNDS]
-    paired = [pair for pair in offsets if len(pair) == 2]
-    firsts, seconds = [pair[0] for pair in paired], [pair[1] for pair in paired]
-    alone = [pair[0] for pair in offsets if len(pair) == 1][0]
-
-    def prepare(k):
-        send_inverse(k).wait_recv()
-        scale_rows(k)
-
-    @pl.loop(0, len(paired))
-    def _(p):
-        @pl.loop(0, 2)
-        def _(side):
-            prepare(jnp.where(side == 0, pick(firsts, p), pick(seconds, p)))
-
-        @pl.when(p >= DEPTH)
+    def factor_of(factors, g):
+        return jnp.concatenate([jnp.broadcast_to(factors[:, a : a + 1], (8, width)) for a in (g, g + 1)], axis=0)
+
+    def scaled(k, e, store):
+        both = inverse[k]
+        factors = jnp.where(e == 0, both, pltpu.roll(both, HALF, 1))
+        for g in range(0, groups, 2):
+            tall = pl.ds(8 * g, 16)
+            merged = wide[k, e, tall, :] + narrow[k, e, tall, :].astype(jnp.float32)
+            store(tall, (merged * factor_of(factors, g)).astype(jnp.bfloat16))
+
+    experts_of, dys_of = [e for e, dy in PIECES], [dy for e, dy in PIECES]
+
+    @pl.loop(0, len(PIECES) * SIDE)
+    def _(i):
+        e, dy, dx = pick(experts_of, i // SIDE), pick(dys_of, i // SIDE), pick(ALONG, i % SIDE)
+        k = dy * SIDE + dx
+
+        @pl.when(k != 0)
         def _():
-            send_rows(pick(firsts, p - DEPTH)).wait_send()
-            send_rows(pick(seconds, p - DEPTH)).wait_send()
-
-        send_rows(pick(firsts, p)).start()
-        send_rows(pick(seconds, p)).start()
-
-    prepare(jnp.int32(alone))
-    late = len(paired) - DEPTH
-    send_rows(firsts[late]).wait_send()
-    send_rows(seconds[late]).wait_send()
-    send_rows(alone).start()
+            @pl.when(e == 0)
+            def _():
+                send_inverse(k).wait_recv()
+
+            def store(tall, value):
+                ready[k, e, tall, :] = value
+
+            scaled(k, e, store)
+
+            @pl.when((dy != 0) & (dx != 0))
+            def _():
+                send_relay(k, e).start()
+
+            @pl.when(((dy == 0) | (dx == 0)) & (e == 0))
+            def _():
+                send_straight(k, 0, True).start()
+
+            @pl.when(((dy == 0) | (dx == 0)) & (e != 0))
+            def _():
+                send_straight(k, 1).start()
 
     @pl.loop(1, shards)
     def _(k):
@@ -215,19 +254,39 @@
     def _(k):
         send_row_router(k).start()
 
+    @pl.loop(0, (len(PIECES) - held) * (SIDE - 1))
+    def _(i):
+        e, dy, dx = pick(experts_of, i // 3), pick(dys_of, i // 3), pick(ALONG, i % 3)
+        k = dy * SIDE + dx
+        send_relay(k, e).wait_recv()
+        forward(k, e).start()
+
     all_router[mine] = row_router[...]
 
-    def keep(e, tall, value):
-        final[e, tall, columns] = value
-
-    scaled(0, keep)
+    @pl.loop(0, held)
+    def _(e):
+        def keep(tall, value):
+            final[e, tall, columns] = value
+
+        scaled(0, e, keep)
+
+    factors = inverse[0]
+
+    @pl.loop(0, len(STRAIGHT))
+    def _(n):
+        send_raw(n, 0).wait_recv()
+        send_raw(n, 1).wait_recv()
+        origin = pl.ds(pl.multiple_of(away(me, pick(STRAIGHT, n)) * width, LANES), width)
+        for g in range(0, CUT[2] // 8, 2):
+            tall = pl.ds(8 * g, 16)
+            final[0, tall, origin] = (raw[n, tall, :] * factor_of(factors, g)).astype(jnp.bfloat16)
 
     for e in range(held):
         for c in range(0, rows, LANES):
             size = min(LANES, rows - c)
             spread = jnp.zeros((8, LANES), jnp.float32)
             for g in range(c // 8, (c + size) // 8):
-                at = e * groups + g
+                at = e * HALF + g
                 spread = jnp.where(lane // 8 == g - c // 8, jnp.broadcast_to(root[:, at : at + 1], (8, LANES)), spread)
             line = jnp.sum(jnp.where(sublane == lane % 8, spread, 0.0), axis=0, keepdims=True)
             scale[e : e + 1, c : c + size] = line[:, :size]
@@ -243,12 +302,21 @@
         send_part(k).wait_send()
         send_inverse(k).wait_send()
         send_router(k).wait_send()
-        send_rows(k).wait_recv()
-
-    for p in range(late + 1, len(paired)):
-        send_rows(firsts[p]).wait_send()
-        send_rows(seconds[p]).wait_send()
-    send_rows(alone).wait_send()
+
+    @pl.loop(0, len(STRAIGHT))
+    def _(n):
+        k = pick(STRAIGHT, n)
+        send_raw(n, 0).wait_send()
+        send_raw(n, 1).wait_send()
+        send_straight(k, 0, True).wait()
+        send_straight(k, 1).wait()
+
+    @pl.loop(0, (len(PIECES) - held) * (SIDE - 1))
+    def _(i):
+        e, dy, dx = pick(experts_of, i // 3), pick(dys_of, i // 3), pick(ALONG, i % 3)
+        k = dy * SIDE + dx
+        send_relay(k, e).wait_send()
+        forward(k, e).wait()
 
 
 def hand_out_kernel(final, scale, router, final_out, scale_out, router_out, final_sem, scale_sem, router_sem):
@@ -304,11 +372,17 @@
                 pltpu.VMEM((experts, held, width * shards), jnp.bfloat16),
                 pltpu.VMEM((held, width), jnp.float32),
                 pltpu.VMEM((1, width), jnp.float32),
+                pltpu.VMEM((len(STRAIGHT), CUT[2], width), jnp.float32),
+                pltpu.VMEM((shards, held, rows, width), jnp.bfloat16),
             ]
             + [dma((shards,))] * 2
             + [dma] * 2
-            + [dma((shards,))] * 8
-            + [dma((experts,))] * 2,
+            + [dma((shards,))] * 4
+            + [dma((held * shards,))] * 2
+            + [dma((shards,))] * 2
+            + [dma((experts,))] * 2
+            + [dma((2 * len(STRAIGHT),))] * 2
+            + [dma((held * shards,))] * 2,
             compiler_params=pltpu.CompilerParams(
                 collective_id=0, has_side_effects=True, vmem_limit_bytes=44 * 1024 * 1024
             ),

time: 99.6 us -> 96.1 us (0.965)
  Pallas kernels: 98.9 us -> 95.3 us
    pallas_call x1, Pallas kernels: 96 us -> 92.4 us  [local(): pl.pallas_call(functools.partial(kernel, shards, experts), name='serve',...]
where the time goes in v2:
time: 96.1 us; the launch traced here: 95.9 us
  Pallas kernels  95.3 us (99%)
    pallas_call x1, Pallas kernels, local(): pl.pallas_call(functools.partial(kernel, shards, experts), name='serve',...  92.4 us
    pallas_call x1, Pallas kernels, hand_out(): pl.pallas_call(hand_out_kernel, name='hand_out', out_shape=tuple((jax.Sha...  2.84 us

profile of v2, /device:TPU:0, one launch (start us, length us, event | category | flops | bytes accessed | tf_op | source)
XLA Modules:
  0.0 95.9 jit_solution(12695414612871830025)
XLA Ops:
  0.6 92.4 %serve.1 = (bf16[2,400,4096]{2,1,0:T(8,128)(2,1)S(1)}, f32[2,400]{1,0:T(2,128)S(1)}, bf16[16,4096]{1,0:T(8,128)(2,1)S(1)}) custom-call(f32[2,6400,256]{2,1,0:T(8,128)} %master.1, bf16[2,6400,256]{2,1,0:T(8,128)(2,1)} %second.1, f32[2,256]{1,0:T(2,128)} %bitcast.3, f32[1,256]{1,0:T(1,128)} %bitcast.4), custom_call_target="tpu_custom_call" | custom-call | tf_op jit(solution)/shard_map/serve/pallas_call | solution.py:353
  93.1 2.8 %hand_out.1 = (bf16[2,400,4096]{2,1,0:T(8,128)(2,1)}, f32[2,400]{1,0:T(2,128)}, bf16[16,4096]{1,0:T(8,128)(2,1)}) custom-call(bf16[2,400,4096]{2,1,0:T(8,128)(2,1)S(1)} %get-tuple-element.9.final, f32[2,400]{1,0:T(2,128)S(1)} %get-tuple-element.10.scale, bf16[16,4096]{1,0:T(8,128)(2,1)S(1)} %get-tuple-element.11.router), custom_call_target="tpu_custom_call" | custom-call | tf_op jit(solution)/shard_map/hand_out/pallas_call | solution.py:335

commit v3 on v0

v3 whole, which is shorter than its diff:
```python
import functools

import jax
import jax.numpy as jnp
from jax import lax
from jax.experimental import pallas as pl
from jax.experimental.pallas import tpu as pltpu
from jax.sharding import PartitionSpec as P

MESH = pl.DeviceIdType.MESH
SIDE = 4
LANES = 128
HALF = LANES // 2
PIECE = 80

RELAYED = ((5, 15, 10), (7, 14, 9), (11, 6, 13))
ALONG_X = (2, 1, 3)
ALONG_Y = (4, 12, 8)
GROUP = tuple(next((n for n, group in enumerate(RELAYED) if k in group), 0) for k in range(SIDE * SIDE))
FIRST = 128
SLOT = FIRST // 8


def pick(table, i):
    value = jnp.int32(table[0])
    for n, entry in enumerate(table[1:], 1):
        value = jnp.where(i == n, jnp.int32(entry), value)
    return value


def toward(shard, k):
    y, x = lax.div(shard, SIDE), lax.rem(shard, SIDE)
    return lax.rem(y + lax.div(k, SIDE), SIDE) * SIDE + lax.rem(x + lax.rem(k, SIDE), SIDE)


def away(shard, k):
    y, x = lax.div(shard, SIDE), lax.rem(shard, SIDE)
    return lax.rem(y + SIDE - lax.div(k, SIDE), SIDE) * SIDE + lax.rem(x + SIDE - lax.rem(k, SIDE), SIDE)


def kernel(
    shards, experts,
    master, second, weight_in, gain_in,
    final, scale, router,
    wide, narrow, ready, stage, first_got, first_total, first_inverse, part, got, rest_total, inverse,
    one_router, row_router, all_router, weight, gain,
    first_read, rest_read, weight_read, gain_read, first_send, first_recv, part_send, part_recv, inv_send, inv_recv,
    rt1_send, rt1_recv, rt2_send, rt2_recv, relay_recv, row_send, forward_send, row_recv,
):
    me = lax.axis_index("shard")
    mine = lax.axis_index("expert")
    held, rows, width = wide.shape[1:]
    columns = pl.ds(pl.multiple_of(me * width, LANES), width)
    chunks = ((0, 0, FIRST), (0, FIRST, rows - FIRST)) + tuple((e, 0, rows) for e in range(1, held))

    def local(ref, sem):
        return pltpu.make_async_copy(ref, ref, sem)

    def read(k, c, sem):
        e, start, count = chunks[c]
        source = pl.ds(pl.multiple_of(toward(me, k) * rows + start, 16), count)
        target = pl.ds(start, count)
        pltpu.make_async_copy(master.at[e, source], wide.at[k, e, target], sem).start()
        pltpu.make_async_copy(second.at[e, source], narrow.at[k, e, target], sem).start()

    read_weight = pltpu.make_async_copy(weight_in, weight, weight_read)
    read_gain = pltpu.make_async_copy(gain_in, gain, gain_read)
    read_weight.start()
    read_gain.start()

    barrier = pltpu.get_barrier_semaphore()

    @pl.loop(1, shards)
    def _(k):
        pl.semaphore_signal(barrier, inc=1, device_id={"shard": toward(me, k)}, device_id_type=MESH)

    @pl.loop(1, experts)
    def _(k):
        pl.semaphore_signal(barrier, inc=1, device_id={"expert": lax.rem(mine + k, experts)}, device_id_type=MESH)

    @pl.loop(0, shards)
    def _(k):
        read(k, 0, first_read)

    @pl.loop(1, shards + 1)
    def _(k):
        for c in range(1, len(chunks)):
            read(lax.rem(k, shards), c, rest_read.at[lax.rem(k, shards)])

    lane = lax.broadcasted_iota(jnp.int32, (8, LANES), 1)
    sublane = lax.broadcasted_iota(jnp.int32, (8, LANES), 0)

    def sums_of(k, c, packed, base):
        e, start, count = chunks[c]
        for g in range(start // 8, (start + count) // 8, 2):
            tall = pl.ds(8 * g, 16)
            merged = wide[k, e, tall, :] + narrow[k, e, tall, :].astype(jnp.float32)
            sums = jnp.sum(merged * merged, axis=1, keepdims=True)
            for h in range(2):
                packed = jnp.where(lane == base + g + h, sums[8 * h : 8 * h + 8], packed)
        return packed

    local(narrow.at[:, 0, pl.ds(0, 3 * FIRST)], first_read).wait()

    def first_sums(i, packed):
        for k in [4 * i + n for n in range(4)]:
            owner = toward(me, k)
            base = lax.rem(owner, 8) * SLOT
            low = owner < 8
            sums = sums_of(k, 0, zero, base)
            packed = packed[0] + jnp.where(low, sums, 0.0), packed[1] + jnp.where(low, 0.0, sums)
        return packed

    zero = jnp.zeros((8, LANES), jnp.float32)
    packed = lax.fori_loop(0, shards // 4, first_sums, (zero, zero))
    first_got[me, 0] = packed[0]
    first_got[me, 1] = packed[1]
    pl.semaphore_wait(barrier, shards + experts - 2)

    @pl.loop(1, shards)
    def _(k):
        pltpu.make_async_remote_copy(
            src_ref=first_got.at[me], dst_ref=first_got.at[me], send_sem=first_send, recv_sem=first_recv,
            device_id={"shard": toward(me, k)}, device_id_type=MESH,
        ).start()

    read_weight.wait()
    read_gain.wait()
    mine_router = (weight[...] * gain[...]).astype(jnp.bfloat16)
    one_router[...] = mine_router
    row_router[:, columns] = mine_router

    @pl.loop(1, shards)
    def _(k):
        pltpu.make_async_remote_copy(
            src_ref=one_router, dst_ref=row_router.at[:, columns], send_sem=rt1_send, recv_sem=rt1_recv,
            device_id={"shard": toward(me, k)}, device_id_type=MESH,
        ).start()

    def rest_sums(k):
        local(narrow.at[pl.ds(0, 3), :, pl.ds(0, (held * rows - FIRST) // held)], rest_read.at[k]).wait()
        packed = zero
        for c in range(1, len(chunks)):
            packed = sums_of(k, c, packed, chunks[c][0] * HALF)
        part[k] = packed

    @pl.loop(1, shards)
    def _(k):
        rest_sums(k)
        pltpu.make_async_remote_copy(
            src_ref=part.at[k], dst_ref=got.at[k], send_sem=part_send, recv_sem=part_recv,
            device_id={"shard": toward(me, k)}, device_id_type=MESH,
        ).start()

    rest_sums(0)

    local(first_got.at[pl.ds(0, shards - 1)], first_recv).wait()
    for v in range(2):
        total = first_got[0, v]
        for d in range(1, shards):
            total += first_got[d, v]
        first_total[v] = total
        first_inverse[v] = 1.0 / jnp.sqrt(total)

    def of_owner(ref, owner):
        return pltpu.roll(ref[lax.div(owner, 8)], LANES - lax.rem(owner, 8) * SLOT, 1)

    def scaled(k, c, store):
        e, start, count = chunks[c]
        factors = of_owner(first_inverse, toward(me, k)) if c == 0 else inverse[k]
        for g in range(start // 8, (start + count) // 8, 2):
            tall = pl.ds(8 * g, 16)
            merged = wide[k, e, tall, :] + narrow[k, e, tall, :].astype(jnp.float32)
            at = [e * HALF + g + h for h in range(2)]
            factor = jnp.concatenate([jnp.broadcast_to(factors[:, a : a + 1], (8, width)) for a in at], axis=0)
            store(e, tall, (merged * factor).astype(jnp.bfloat16))

    def send_pieces(c, offsets):
        e, start, count = chunks[c]
        part_rows = pl.ds(start, count)

        @pl.loop(0, len(offsets))
        def _(i):
            k = pick(offsets, i)
            dy, dx = lax.div(k, SIDE), lax.rem(k, SIDE)

            if c == held:
                local(inverse.at[k], inv_recv.at[k]).wait()

            def store(e, tall, value):
                ready[k, e, tall, :] = value

            scaled(k, c, store)

            @pl.when((dy != 0) & (dx != 0))
            def _():
                pltpu.make_async_remote_copy(
                    src_ref=ready.at[k, e, part_rows], dst_ref=stage.at[k, e, part_rows],
                    send_sem=row_send, recv_sem=relay_recv.at[c * SIDE + pick(GROUP, k)],
                    device_id={"shard": toward(me, dx)}, device_id_type=MESH,
                ).start()

            @pl.when((dy == 0) | (dx == 0))
            def _():
                pltpu.make_async_remote_copy(
                    src_ref=ready.at[k, e, part_rows], dst_ref=final.at[e, part_rows, columns],
                    send_sem=row_send, recv_sem=row_recv,
                    device_id={"shard": toward(me, k)}, device_id_type=MESH,
                ).start()

    def forward_groups(c, begin, end):
        e, start, count = chunks[c]
        part_rows = pl.ds(start, count)

        @pl.loop(begin, end)
        def _(i):
            local(stage.at[pl.ds(0, SIDE - 1), e, part_rows], relay_recv.at[c * SIDE + i]).wait()

            @pl.loop(0, SIDE - 1)
            def _(j):
                k = pick(sum(RELAYED, ()), i * (SIDE - 1) + j)
                origin = pl.ds(pl.multiple_of(away(me, lax.rem(k, SIDE)) * width, LANES), width)
                pltpu.make_async_remote_copy(
                    src_ref=stage.at[k, e, part_rows], dst_ref=final.at[e, part_rows, origin],
                    send_sem=forward_send, recv_sem=row_recv,
                    device_id={"shard": toward(me, k - lax.rem(k, SIDE))}, device_id_type=MESH,
                ).start()

    send_pieces(0, RELAYED[0] + ALONG_Y)

    local(got.at[pl.ds(1, shards - 1)], part_recv).wait()
    total = part[0]
    for k in range(1, shards):
        total += got[k]
    rest_total[...] = total
    inverse[0] = 1.0 / jnp.sqrt(total)

    @pl.loop(1, shards)
    def _(k):
        pltpu.make_async_remote_copy(
            src_ref=inverse.at[0], dst_ref=inverse.at[k], send_sem=inv_send, recv_sem=inv_recv.at[k],
            device_id={"shard": away(me, k)}, device_id_type=MESH,
        ).start()

    send_pieces(0, RELAYED[1] + RELAYED[2] + ALONG_X)
    others = row_router.at[:, pl.ds(0, (shards - 1) * width)]
    local(others, rt1_recv).wait()

    @pl.loop(1, experts)
    def _(k):
        pltpu.make_async_remote_copy(
            src_ref=row_router, dst_ref=all_router.at[mine], send_sem=rt2_send, recv_sem=rt2_recv,
            device_id={"expert": lax.rem(mine + k, experts)}, device_id_type=MESH,
        ).start()

    all_router[mine] = row_router[...]

    forward_groups(0, 0, 3)
    late = range(len(chunks) - 1, 0, -1)
    for c in late:
        send_pieces(c, RELAYED[0] + ALONG_Y + RELAYED[1] + RELAYED[2])

    for c in late[:-1]:
        forward_groups(c, 0, 3)
    forward_groups(late[-1], 0, 2)
    for c in late:
        send_pieces(c, ALONG_X)
    forward_groups(late[-1], 2, 3)

    def keep(e, tall, value):
        final[e, tall, columns] = value

    for c in range(len(chunks)):
        scaled(0, c, keep)

    root = jnp.sqrt(jnp.where(lane < SLOT, of_owner(first_total, me), rest_total[...]))
    for e in range(held):
        for c in range(0, rows, LANES):
            size = min(LANES, rows - c)
            spread = jnp.zeros((8, LANES), jnp.float32)
            for g in range(c // 8, (c + size) // 8):
                at = e * HALF + g
                spread = jnp.where(lane // 8 == g - c // 8, jnp.broadcast_to(root[:, at : at + 1], (8, LANES)), spread)
            line = jnp.sum(jnp.where(sublane == lane % 8, spread, 0.0), axis=0, keepdims=True)
            scale[e : e + 1, c : c + size] = line[:, :size]

    local(all_router.at[pl.ds(0, experts - 1)], rt2_recv).wait()
    router[...] = all_router[...].reshape(router.shape)

    local(first_got.at[pl.ds(0, shards - 1)], first_send).wait()
    local(part.at[pl.ds(1, shards - 1)], part_send).wait()
    local(got.at[pl.ds(1, shards - 1)], inv_send).wait()
    local(others, rt1_send).wait()
    local(all_router.at[pl.ds(0, experts - 1)], rt2_send).wait()
    local(ready.at[pl.ds(1, shards - 1)], row_send).wait()
    local(ready.at[pl.ds(0, (SIDE - 1) * (SIDE - 1))], forward_send).wait()
    local(ready.at[pl.ds(1, shards - 1)], row_recv).wait()


def hand_out_kernel(final, scale, router, final_out, scale_out, router_out, sem):
    copies = [(scale, scale_out), (router, router_out)]
    held, rows, _ = final.shape
    for e in range(held):
        for start in range(0, rows, PIECE):
            at = (e, pl.ds(start, min(PIECE, rows - start)))
            copies.append((final.at[at], final_out.at[at]))
    copies = [pltpu.make_async_copy(source, target, sem.at[n]) for n, (source, target) in enumerate(copies)]
    for copy in copies:
        copy.start()
    for copy in copies:
        copy.wait()


def hand_out(*arrays):
    held, rows, _ = arrays[0].shape
    return pl.pallas_call(
        hand_out_kernel,
        name="hand_out",
        out_shape=tuple(jax.ShapeDtypeStruct(x.shape, x.dtype) for x in arrays),
        in_specs=[pl.BlockSpec(memory_space=pltpu.VMEM)] * 3,
        out_specs=(pl.BlockSpec(memory_space=pltpu.HBM),) * 3,
        scratch_shapes=[pltpu.SemaphoreType.DMA((2 + held * pl.cdiv(rows, PIECE),))],
        compiler_params=pltpu.CompilerParams(vmem_limit_bytes=8 * 1024 * 1024),
    )(*arrays)


def solution(mesh):
    shards, experts = mesh.shape["shard"], mesh.shape["expert"]

    def local(master, second, weight, gain):
        held, length, width = master.shape
        rows = length // shards
        dma = pltpu.SemaphoreType.DMA
        wide = (shards, held, rows, width)
        final, scale, router = pl.pallas_call(
            functools.partial(kernel, shards, experts),
            name="serve",
            out_shape=(
                jax.ShapeDtypeStruct((held, rows, width * shards), jnp.bfloat16),
                jax.ShapeDtypeStruct((held, rows), jnp.float32),
                jax.ShapeDtypeStruct((experts * held, width * shards), jnp.bfloat16),
            ),
            in_specs=[pl.BlockSpec(memory_space=pltpu.HBM)] * 4,
            out_specs=(pl.BlockSpec(memory_space=pltpu.VMEM),) * 3,
            scratch_shapes=[
                pltpu.VMEM(wide, jnp.float32),
                pltpu.VMEM(wide, jnp.bfloat16),
                pltpu.VMEM(wide, jnp.bfloat16),
                pltpu.VMEM(wide, jnp.bfloat16),
                pltpu.VMEM((shards, 2, 8, LANES), jnp.float32),
                pltpu.VMEM((2, 8, LANES), jnp.float32),
                pltpu.VMEM((2, 8, LANES), jnp.float32),
                pltpu.VMEM((shards, 8, LANES), jnp.float32),
                pltpu.VMEM((shards, 8, LANES), jnp.float32),
                pltpu.VMEM((8, LANES), jnp.float32),
                pltpu.VMEM((shards, 8, LANES), jnp.float32),
                pltpu.VMEM((held, width), jnp.bfloat16),
                pltpu.VMEM((held, width * shards), jnp.bfloat16),
                pltpu.VMEM((experts, held, width * shards), jnp.bfloat16),
                pltpu.VMEM((held, width), jnp.float32),
                pltpu.VMEM((1, width), jnp.float32),
                dma, dma((shards,)), dma, dma, dma, dma, dma, dma, dma, dma((shards,)),
                dma, dma, dma, dma, dma(((held + 1) * SIDE,)), dma, dma, dma,
            ],
            compiler_params=pltpu.CompilerParams(
                collective_id=0, has_side_effects=True, vmem_limit_bytes=44 * 1024 * 1024
            ),
        )(*[pltpu.with_memory_space_constraint(x, pltpu.HBM) for x in (master, second, weight.T, gain[None, :])])
        final, scale, router = hand_out(final, scale, router)
        return final, scale, router.T

    return jax.shard_map(
        local,
        mesh=mesh,
        in_specs=(P("expert", None, "shard"), P("expert", None, "shard"), P("shard", "expert"), P("shard")),
        out_specs=(P("expert", "shard", None), P("expert", "shard"), P()),
        check_vma=False,
    )
```

time: 156 us -> 92 us (0.59)
  Pallas kernels: 0 us -> 91.2 us
  waiting for transfers between devices: 84.3 us -> 0 us
  starting transfers between devices: 22.3 us -> 0 us
  other arithmetic: 18.9 us -> 0 us
  blocking collectives: 15 us -> 0 us
  local copies, waits for them, and re-layouts: 14.8 us -> 0 us
    pallas_call x0 -> x2, Pallas kernels: none -> 91.2 us  [the longest x1 88.3 us: local(): pl.pallas_call(functools.partial(kernel, shards, experts), name='serve',...]
    all_to_all x4 -> x0, waiting for transfers between devices: 84.3 us -> none  [the longest x2 69.4 us: several_exchanges(): lax.all_to_all(share, axis, split_axis=0, concat_axis=0, tiled=True)]
    all_to_all x4 -> x0, starting transfers between devices: 22.3 us -> none  [the longest x2 11.6 us: several_exchanges(): lax.all_to_all(share, axis, split_axis=0, concat_axis=0, tiled=True)]
    all_gather x2 -> x0, blocking collectives: 15 us -> none  [all_blocks(): parts = lax.all_gather(parts, axes[k])]
    reduce_sum x2 -> x0, other arithmetic: 8.7 us -> none  [the longest x1 8.44 us: local(): jnp.sum(merged_down * merged_down, axis=2)]
    split x3 -> x0, local copies, waits for them, and re-layouts: 7.89 us -> none  [several_exchanges(): jnp.split(parts, cut_rows(parts.shape[widest], pieces), axis=widest)]
    convert_element_type x2 -> x0, other arithmetic: 7.74 us -> none  [the longest x1 7.74 us: local(): (merged_down / jnp.expand_dims(scale_down, 2)).astype(jnp.bfloat16)]
    reshape x2 -> x0, local copies, waits for them, and re-layouts: 4.4 us -> none  [joined_along(): parts.reshape(*shape[:dim], shape[dim] * shape[dim + 1], *shape[dim + 2:])]
  transfers between devices with their start and end apart: 4 -> 0, of which waited for: 3 -> 0; matrix products, arithmetic and copies ran while one was open for 11% -> 0% of each run, Pallas kernels for 0% -> 0%
where the time goes in v3:
time: 92 us; the launch traced here: 91.9 us
  Pallas kernels  91.2 us (99%)
    pallas_call x1, Pallas kernels, local(): pl.pallas_call(functools.partial(kernel, shards, experts), name='serve',...  88.3 us
    pallas_call x1, Pallas kernels, hand_out(): pl.pallas_call(hand_out_kernel, name='hand_out', out_shape=tuple((jax.Sha...  2.89 us

profile of v3, /device:TPU:0, one launch (start us, length us, event | category | flops | bytes accessed | tf_op | source)
XLA Modules:
  0.0 91.9 jit_solution(9597436271121243933)
XLA Ops:
  0.6 88.3 %serve.1 = (bf16[2,400,4096]{2,1,0:T(8,128)(2,1)S(1)}, f32[2,400]{1,0:T(2,128)S(1)}, bf16[16,4096]{1,0:T(8,128)(2,1)S(1)}) custom-call(f32[2,6400,256]{2,1,0:T(8,128)} %master.1, bf16[2,6400,256]{2,1,0:T(8,128)(2,1)} %second.1, f32[2,256]{1,0:T(2,128)} %bitcast.3, f32[1,256]{1,0:T(1,128)} %bitcast.4), custom_call_target="tpu_custom_call" | custom-call | tf_op jit(solution)/shard_map/serve/pallas_call | solution.py:335
  89.0 2.9 %hand_out.1 = (bf16[2,400,4096]{2,1,0:T(8,128)(2,1)}, f32[2,400]{1,0:T(2,128)}, bf16[16,4096]{1,0:T(8,128)(2,1)}) custom-call(bf16[2,400,4096]{2,1,0:T(8,128)(2,1)S(1)} %get-tuple-element.9.final, f32[2,400]{1,0:T(2,128)S(1)} %get-tuple-element.10.scale, bf16[16,4096]{1,0:T(8,128)(2,1)S(1)} %get-tuple-element.11.router), custom_call_target="tpu_custom_call" | custom-call | tf_op jit(solution)/shard_map/hand_out/pallas_call | solution.py:316

commit v4 on v3

--- a/solution.py
+++ b/solution.py
@@ -14,6 +14,7 @@
 PIECE = 80
 
 RELAYED = ((5, 15, 10), (7, 14, 9), (11, 6, 13))
+Y_FIRST = ((1,), (1,), (1,))
 ALONG_X = (2, 1, 3)
 ALONG_Y = (4, 12, 8)
 GROUP = tuple(next((n for n, group in enumerate(RELAYED) if k in group), 0) for k in range(SIDE * SIDE))
@@ -175,6 +176,10 @@
             factor = jnp.concatenate([jnp.broadcast_to(factors[:, a : a + 1], (8, width)) for a in at], axis=0)
             store(e, tall, (merged * factor).astype(jnp.bfloat16))
 
+    def first_hop(c, k):
+        swapped = sum([RELAYED[n] for n in Y_FIRST[c]], ())
+        return pick([n - n % SIDE if n in swapped else n % SIDE for n in range(shards)], k)
+
     def send_pieces(c, offsets):
         e, start, count = chunks[c]
         part_rows = pl.ds(start, count)
@@ -197,7 +202,7 @@
                 pltpu.make_async_remote_copy(
                     src_ref=ready.at[k, e, part_rows], dst_ref=stage.at[k, e, part_rows],
                     send_sem=row_send, recv_sem=relay_recv.at[c * SIDE + pick(GROUP, k)],
-                    device_id={"shard": toward(me, dx)}, device_id_type=MESH,
+                    device_id={"shard": toward(me, first_hop(c, k))}, device_id_type=MESH,
                 ).start()
 
             @pl.when((dy == 0) | (dx == 0))
@@ -219,11 +224,12 @@
             @pl.loop(0, SIDE - 1)
             def _(j):
                 k = pick(sum(RELAYED, ()), i * (SIDE - 1) + j)
-                origin = pl.ds(pl.multiple_of(away(me, lax.rem(k, SIDE)) * width, LANES), width)
+                hop = first_hop(c, k)
+                origin = pl.ds(pl.multiple_of(away(me, hop) * width, LANES), width)
                 pltpu.make_async_remote_copy(
                     src_ref=stage.at[k, e, part_rows], dst_ref=final.at[e, part_rows, origin],
                     send_sem=forward_send, recv_sem=row_recv,
-                    device_id={"shard": toward(me, k - lax.rem(k, SIDE))}, device_id_type=MESH,
+                    device_id={"shard": toward(me, k - hop)}, device_id_type=MESH,
                 ).start()
 
     send_pieces(0, RELAYED[0] + ALONG_Y)

time: 92 us -> 89.8 us (0.976)
  Pallas kernels: 91.2 us -> 89 us
    pallas_call x1, Pallas kernels: 88.3 us -> 86.1 us  [local(): pl.pallas_call(functools.partial(kernel, shards, experts), name='serve',...]
where the time goes in v4:
time: 89.8 us; the launch traced here: 89.7 us
  Pallas kernels  89 us (99%)
    pallas_call x1, Pallas kernels, local(): pl.pallas_call(functools.partial(kernel, shards, experts), name='serve',...  86.1 us
    pallas_call x1, Pallas kernels, hand_out(): pl.pallas_call(hand_out_kernel, name='hand_out', out_shape=tuple((jax.Sha...  2.89 us

profile of v4, /device:TPU:0, one launch (start us, length us, event | category | flops | bytes accessed | tf_op | source)
XLA Modules:
  0.0 89.7 jit_solution(817785504932393301)
XLA Ops:
  0.6 86.1 %serve.1 = (bf16[2,400,4096]{2,1,0:T(8,128)(2,1)S(1)}, f32[2,400]{1,0:T(2,128)S(1)}, bf16[16,4096]{1,0:T(8,128)(2,1)S(1)}) custom-call(f32[2,6400,256]{2,1,0:T(8,128)} %master.1, bf16[2,6400,256]{2,1,0:T(8,128)(2,1)} %second.1, f32[2,256]{1,0:T(2,128)} %bitcast.3, f32[1,256]{1,0:T(1,128)} %bitcast.4), custom_call_target="tpu_custom_call" | custom-call | tf_op jit(solution)/shard_map/serve/pallas_call | solution.py:341
  86.8 2.9 %hand_out.1 = (bf16[2,400,4096]{2,1,0:T(8,128)(2,1)}, f32[2,400]{1,0:T(2,128)}, bf16[16,4096]{1,0:T(8,128)(2,1)}) custom-call(bf16[2,400,4096]{2,1,0:T(8,128)(2,1)S(1)} %get-tuple-element.9.final, f32[2,400]{1,0:T(2,128)S(1)} %get-tuple-element.10.scale, bf16[16,4096]{1,0:T(8,128)(2,1)S(1)} %get-tuple-element.11.router), custom_call_target="tpu_custom_call" | custom-call | tf_op jit(solution)/shard_map/hand_out/pallas_call | solution.py:322

commit v5 on v4

--- a/solution.py
+++ b/solution.py
@@ -71,11 +71,11 @@
 
     barrier = pltpu.get_barrier_semaphore()
 
-    @pl.loop(1, shards)
+    @pl.loop(1, shards, unroll=True)
     def _(k):
         pl.semaphore_signal(barrier, inc=1, device_id={"shard": toward(me, k)}, device_id_type=MESH)
 
-    @pl.loop(1, experts)
+    @pl.loop(1, experts, unroll=True)
     def _(k):
         pl.semaphore_signal(barrier, inc=1, device_id={"expert": lax.rem(mine + k, experts)}, device_id_type=MESH)
 
@@ -118,7 +118,7 @@
     first_got[me, 1] = packed[1]
     pl.semaphore_wait(barrier, shards + experts - 2)
 
-    @pl.loop(1, shards)
+    @pl.loop(1, shards, unroll=True)
     def _(k):
         pltpu.make_async_remote_copy(
             src_ref=first_got.at[me], dst_ref=first_got.at[me], send_sem=first_send, recv_sem=first_recv,
@@ -164,7 +164,7 @@
         first_inverse[v] = 1.0 / jnp.sqrt(total)
 
     def of_owner(ref, owner):
-        return pltpu.roll(ref[lax.div(owner, 8)], LANES - lax.rem(owner, 8) * SLOT, 1)
+        return pltpu.roll(ref[lax.div(owner, 8)], lax.rem(LANES - lax.rem(owner, 8) * SLOT, LANES), 1)
 
     def scaled(k, c, store):
         e, start, count = chunks[c]

time: 89.8 us -> 89.6 us (level)
  no operation moved by 1% of the time
where the time goes in v5:
time: 89.6 us; the launch traced here: 89.5 us
  Pallas kernels  88.8 us (99%)
    pallas_call x1, Pallas kernels, local(): pl.pallas_call(functools.partial(kernel, shards, experts), name='serve',...  85.9 us
    pallas_call x1, Pallas kernels, hand_out(): pl.pallas_call(hand_out_kernel, name='hand_out', out_shape=tuple((jax.Sha...  2.89 us

profile of v5, /device:TPU:0, one launch (start us, length us, event | category | flops | bytes accessed | tf_op | source)
XLA Modules:
  0.0 89.5 jit_solution(12502271332970230639)
XLA Ops:
  0.6 85.9 %serve.1 = (bf16[2,400,4096]{2,1,0:T(8,128)(2,1)S(1)}, f32[2,400]{1,0:T(2,128)S(1)}, bf16[16,4096]{1,0:T(8,128)(2,1)S(1)}) custom-call(f32[2,6400,256]{2,1,0:T(8,128)} %master.1, bf16[2,6400,256]{2,1,0:T(8,128)(2,1)} %second.1, f32[2,256]{1,0:T(2,128)} %bitcast.3, f32[1,256]{1,0:T(1,128)} %bitcast.4), custom_call_target="tpu_custom_call" | custom-call | tf_op jit(solution)/shard_map/serve/pallas_call | solution.py:341
  86.6 2.9 %hand_out.1 = (bf16[2,400,4096]{2,1,0:T(8,128)(2,1)}, f32[2,400]{1,0:T(2,128)}, bf16[16,4096]{1,0:T(8,128)(2,1)}) custom-call(bf16[2,400,4096]{2,1,0:T(8,128)(2,1)S(1)} %get-tuple-element.9.final, f32[2,400]{1,0:T(2,128)S(1)} %get-tuple-element.10.scale, bf16[16,4096]{1,0:T(8,128)(2,1)S(1)} %get-tuple-element.11.router), custom_call_target="tpu_custom_call" | custom-call | tf_op jit(solution)/shard_map/hand_out/pallas_call | solution.py:322

commit v6 on v5

--- a/solution.py
+++ b/solution.py
@@ -189,9 +189,6 @@
             k = pick(offsets, i)
             dy, dx = lax.div(k, SIDE), lax.rem(k, SIDE)
 
-            if c == held:
-                local(inverse.at[k], inv_recv.at[k]).wait()
-
             def store(e, tall, value):
                 ready[k, e, tall, :] = value
 
@@ -244,7 +241,7 @@
     @pl.loop(1, shards)
     def _(k):
         pltpu.make_async_remote_copy(
-            src_ref=inverse.at[0], dst_ref=inverse.at[k], send_sem=inv_send, recv_sem=inv_recv.at[k],
+            src_ref=inverse.at[0], dst_ref=inverse.at[k], send_sem=inv_send, recv_sem=inv_recv,
             device_id={"shard": away(me, k)}, device_id_type=MESH,
         ).start()
 
@@ -262,6 +259,7 @@
     all_router[mine] = row_router[...]
 
     forward_groups(0, 0, 3)
+    local(inverse.at[pl.ds(1, shards - 1)], inv_recv).wait()
     late = range(len(chunks) - 1, 0, -1)
     for c in late:
         send_pieces(c, RELAYED[0] + ALONG_Y + RELAYED[1] + RELAYED[2])
@@ -365,7 +363,7 @@
                 pltpu.VMEM((experts, held, width * shards), jnp.bfloat16),
                 pltpu.VMEM((held, width), jnp.float32),
                 pltpu.VMEM((1, width), jnp.float32),
-                dma, dma((shards,)), dma, dma, dma, dma, dma, dma, dma, dma((shards,)),
+                dma, dma((shards,)), dma, dma, dma, dma, dma, dma, dma, dma,
                 dma, dma, dma, dma, dma(((held + 1) * SIDE,)), dma, dma, dma,
             ],
             compiler_params=pltpu.CompilerParams(

time: 89.6 us -> 89.4 us (level)
  no operation moved by 1% of the time
where the time goes in v6:
time: 89.4 us; the launch traced here: 89.3 us
  Pallas kernels  88.7 us (99%)
    pallas_call x1, Pallas kernels, local(): pl.pallas_call(functools.partial(kernel, shards, experts), name='serve',...  85.8 us
    pallas_call x1, Pallas kernels, hand_out(): pl.pallas_call(hand_out_kernel, name='hand_out', out_shape=tuple((jax.Sha...  2.89 us

profile of v6, /device:TPU:0, one launch (start us, length us, event | category | flops | bytes accessed | tf_op | source)
XLA Modules:
  0.0 89.3 jit_solution(16458280278526542758)
XLA Ops:
  0.6 85.8 %serve.1 = (bf16[2,400,4096]{2,1,0:T(8,128)(2,1)S(1)}, f32[2,400]{1,0:T(2,128)S(1)}, bf16[16,4096]{1,0:T(8,128)(2,1)S(1)}) custom-call(f32[2,6400,256]{2,1,0:T(8,128)} %master.1, bf16[2,6400,256]{2,1,0:T(8,128)(2,1)} %second.1, f32[2,256]{1,0:T(2,128)} %bitcast.3, f32[1,256]{1,0:T(1,128)} %bitcast.4), custom_call_target="tpu_custom_call" | custom-call | tf_op jit(solution)/shard_map/serve/pallas_call | solution.py:339
  86.4 2.9 %hand_out.1 = (bf16[2,400,4096]{2,1,0:T(8,128)(2,1)}, f32[2,400]{1,0:T(2,128)}, bf16[16,4096]{1,0:T(8,128)(2,1)}) custom-call(bf16[2,400,4096]{2,1,0:T(8,128)(2,1)S(1)} %get-tuple-element.9.final, f32[2,400]{1,0:T(2,128)S(1)} %get-tuple-element.10.scale, bf16[16,4096]{1,0:T(8,128)(2,1)S(1)} %get-tuple-element.11.router), custom_call_target="tpu_custom_call" | custom-call | tf_op jit(solution)/shard_map/hand_out/pallas_call | solution.py:320
